TPU v7x, 32 devices: a whole 2x2x4 slice. The times are simulated.
32 devices in a mesh: dp: 16 (over z, y, x), seq: 2 (over core).
Axes of the slice: x: 2, y: 2, z: 4, core: 2. Of those that a mesh axis runs over, the one named last changes fastest.
Arguments:
- chains_in: bfloat16 [128, 160, 768], P(('dp', 'seq')), may hold values from -6 to 6
- lengths: int32 [128], P(('dp', 'seq')), may hold values from 95 to 160
- d_out: bfloat16 [128, 160, 768], P(('dp', 'seq')), may hold values from -6 to 6
- w_query: bfloat16 [768, 768], replicated, may hold values from -0.21875 to 0.21875
- b_query: float32 [768], replicated, may hold values from -3 to 3
- w_key: bfloat16 [768, 768], replicated, may hold values from -0.21875 to 0.21875
- w_value: bfloat16 [768, 768], replicated, may hold values from -0.21875 to 0.21875
- b_value: float32 [768], replicated, may hold values from -3 to 3
- w_output: bfloat16 [768, 768], replicated, may hold values from -2.5 to 2.5
- b_output: float32 [768], replicated, may hold values from -3 to 3
- gain_one: float32 [768], replicated, may hold values from 0.25 to 1.75
- shift_one: float32 [768], replicated, may hold values from -2 to 2
- w_inner: bfloat16 [768, 3072], replicated, may hold values from -0.21875 to 0.21875
- b_inner: float32 [3072], replicated, may hold values from -3 to 3
- w_outer: bfloat16 [3072, 768], replicated, may hold values from -0.109375 to 0.109375
- b_outer: float32 [768], replicated, may hold values from -3 to 3
- gain_two: float32 [768], replicated, may hold values from 0.25 to 1.75
- shift_two: float32 [768], replicated, may hold values from -2 to 2
Outputs:
- layer_out: bfloat16 [128, 160, 768], P(('dp', 'seq'))
- d_x: float32 [128, 160, 768], P(('dp', 'seq'))
- d_w_query: float32 [768, 768], replicated
- d_b_query: float32 [768], replicated
- d_w_key: float32 [768, 768], replicated
- d_w_value: float32 [768, 768], replicated
- d_b_value: float32 [768], replicated
- d_w_output: float32 [768, 768], replicated
- d_b_output: float32 [768], replicated
- d_gain_one: float32 [768], replicated
- d_shift_one: float32 [768], replicated
- d_w_inner: float32 [768, 3072], replicated
- d_b_inner: float32 [3072], replicated
- d_w_outer: float32 [3072, 768], replicated
- d_b_outer: float32 [768], replicated
- d_gain_two: float32 [768], replicated
- d_shift_two: float32 [768], replicated
Inputs may be any that keep to these rules, and one draw needn't show every extreme that they name: `lengths`: every chain fills more than half of its 160 positions.
All inputs are finite; a program needn't handle non-finite values.
Results may differ from a plain program's by a relative error of at most 0.015.
Values may be sent and summed in bfloat16 or wider, within the bound.
No kernel may reach another device: no remote copies, remote signals or barrier semaphores. Data moves between devices by JAX's collectives and lax.ppermute only.
A program may use at most 256 MiB of HBM per device.

v0:
```python
import jax
import jax.numpy as jnp
from jax import lax
from jax.sharding import PartitionSpec as P

H = 12
EPS = 1e-12


def norm_forward(h, gain, shift):
    centre = h - jnp.mean(h, -1, keepdims=True)
    scale = lax.rsqrt(jnp.mean(centre * centre, -1, keepdims=True) + EPS)
    unit = centre * scale
    return (unit * gain + shift, unit, scale)


def norm_backward(grad, unit, scale, gain):
    d_gain = jnp.sum(grad * unit, 0)
    d_shift = jnp.sum(grad, 0)
    inner = grad * gain
    d_h = scale * (
        inner
        - jnp.mean(inner, -1, keepdims=True)
        - unit * jnp.mean(inner * unit, -1, keepdims=True)
    )
    return (d_h, d_gain, d_shift)


def over_rows(left, right):
    return lax.dot_general(
        left, right, (((0,), (0,)), ((), ())), preferred_element_type=jnp.float32
    )


def times_trans(left, weight):
    return lax.dot_general(
        left, weight, (((1,), (1,)), ((), ())), preferred_element_type=jnp.float32
    )


def attn_scores(query, keys, live_keys):
    seqs, count, width = query.shape
    total = keys.shape[1]
    size = width // H
    q_heads = query.reshape(seqs, count, H, size)
    k_heads = keys.reshape(seqs, total, H, size)
    scores = (
        jnp.einsum("bqhe,bkhe->bhqk", q_heads, k_heads, preferred_element_type=jnp.float32) * 0.125
    )
    return jnp.where(live_keys[:, None, None, :], scores, -1000000000.0)


def packed(grads, count):
    flat = jnp.concatenate([g.reshape(-1) for g in grads])
    extra = -flat.shape[0] % count
    return flat.reshape(count, -1)


def unpacked(flat, grads):
    flat = flat.reshape(-1)
    pieces = []
    start = 0
    for grad in grads:
        number = grad.size
        pieces.append(flat[start : start + number].reshape(grad.shape))
        start = start + number
    return tuple(pieces)


def body(
    chains_in,
    lengths,
    d_out,
    w_query,
    b_query,
    w_key,
    w_value,
    b_value,
    w_output,
    b_output,
    gain_one,
    shift_one,
    w_inner,
    b_inner,
    w_outer,
    b_outer,
    gain_two,
    shift_two,
):
    f32 = jnp.float32
    low_type = jnp.bfloat16
    seqs, length, width = chains_in.shape
    rows = seqs * length
    size = width // H
    parts = lax.axis_size("dp")
    count = lax.axis_size("dp") * lax.axis_size("seq")
    place = jnp.arange(length, dtype=jnp.int32)
    live_rows = place[None, :] < lengths[:, None]
    flat_x = chains_in.reshape(rows, width)
    query = (
        (jnp.dot(flat_x, w_query, preferred_element_type=f32) + b_query)
        .astype(low_type)
        .reshape(seqs, length, width)
    )
    keys = (
        jnp.dot(flat_x, w_key, preferred_element_type=f32)
        .astype(low_type)
        .reshape(seqs, length, width)
    )
    values = (
        (jnp.dot(flat_x, w_value, preferred_element_type=f32) + b_value)
        .astype(low_type)
        .reshape(seqs, length, width)
    )
    scores = attn_scores(query, keys, live_rows)
    top = jnp.max(scores, -1, keepdims=True)
    expo = jnp.exp(scores - top)
    summed = jnp.sum(expo, -1, keepdims=True)
    prob_b = (expo / summed).astype(low_type)
    lse = top + jnp.log(summed)
    v_heads = values.reshape(seqs, length, H, size)
    mixed = (
        jnp.einsum("bhqk,bkhe->bqhe", prob_b, v_heads, preferred_element_type=f32)
        .reshape(rows, width)
        .astype(low_type)
    )
    h_one = flat_x.astype(f32) + jnp.dot(mixed, w_output, preferred_element_type=f32) + b_output
    first, unit_one, scale_one = norm_forward(h_one, gain_one, shift_one)
    live_flat = live_rows.reshape(rows)
    fin = first.astype(low_type)
    pre = jnp.dot(fin, w_inner, preferred_element_type=f32) + b_inner
    hidden = jax.nn.gelu(pre, approximate=False).astype(low_type)
    ffn_home = (jnp.dot(hidden, w_outer, preferred_element_type=f32) + b_outer).astype(low_type)
    h_two = first + ffn_home.astype(f32)
    second, unit_two, scale_two = norm_forward(h_two, gain_two, shift_two)
    keep = live_flat[:, None].astype(f32)
    layer_out = (second * keep).astype(low_type).reshape(seqs, length, width)
    grad_out = d_out.reshape(rows, width).astype(f32) * keep
    d_h_two, d_gain_two, d_shift_two = norm_backward(grad_out, unit_two, scale_two, gain_two)
    d_ffn = d_h_two.astype(low_type)
    d_w_outer = over_rows(hidden, d_ffn)
    d_b_outer = jnp.sum(d_ffn.astype(f32), 0)
    d_hidden = times_trans(d_ffn, w_outer)
    gelu_pull = jax.vjp(lambda z: jax.nn.gelu(z, approximate=False), pre)[1]
    d_pre = gelu_pull(d_hidden)[0].astype(low_type)
    d_w_inner = over_rows(fin, d_pre)
    d_b_inner = jnp.sum(d_pre.astype(f32), 0)
    d_fin = times_trans(d_pre, w_inner).astype(low_type)
    d_home = d_fin
    d_first = d_h_two + d_home.astype(f32)
    ffn_grads = (d_w_inner, d_b_inner, d_w_outer, d_b_outer, d_gain_two, d_shift_two)
    d_h_one, d_gain_one, d_shift_one = norm_backward(d_first, unit_one, scale_one, gain_one)
    d_attn = d_h_one.astype(low_type)
    d_w_output = over_rows(mixed, d_attn)
    d_b_output = jnp.sum(d_attn.astype(f32), 0)
    d_mixed = times_trans(d_attn, w_output).astype(low_type).reshape(seqs, length, H, size)
    scores = attn_scores(query, keys, live_rows)
    prob = jnp.exp(scores - lse)
    prob_b = prob.astype(low_type)
    d_prob = jnp.einsum("bqhe,bkhe->bhqk", d_mixed, v_heads, preferred_element_type=f32)
    delta = jnp.sum(prob * d_prob, -1, keepdims=True)
    d_scores = (prob * (d_prob - delta)).astype(low_type)
    k_heads = keys.reshape(seqs, length, H, size)
    q_heads = query.reshape(seqs, length, H, size)
    d_query = (
        (jnp.einsum("bhqk,bkhe->bqhe", d_scores, k_heads, preferred_element_type=f32) * 0.125)
        .astype(low_type)
        .reshape(rows, width)
    )
    d_key = (
        (jnp.einsum("bhqk,bqhe->bkhe", d_scores, q_heads, preferred_element_type=f32) * 0.125)
        .astype(low_type)
        .reshape(rows, width)
    )
    d_value = (
        jnp.einsum("bhqk,bqhe->bkhe", prob_b, d_mixed, preferred_element_type=f32)
        .astype(low_type)
        .reshape(rows, width)
    )
    d_w_query = over_rows(flat_x, d_query)
    d_b_query = jnp.sum(d_query.astype(f32), 0)
    d_w_key = over_rows(flat_x, d_key)
    d_w_value = over_rows(flat_x, d_value)
    d_b_value = jnp.sum(d_value.astype(f32), 0)
    d_x = (
        d_h_one
        + times_trans(d_query, w_query)
        + times_trans(d_key, w_key)
        + times_trans(d_value, w_value)
    )
    d_x = d_x.reshape(seqs, length, width)
    attn_grads = (
        d_w_query,
        d_b_query,
        d_w_key,
        d_w_value,
        d_b_value,
        d_w_output,
        d_b_output,
        d_gain_one,
        d_shift_one,
    )
    local_grads = attn_grads + ffn_grads
    big = [g for g in local_grads if g.ndim == 2]
    small = [g for g in local_grads if g.ndim == 1]
    sums = lax.psum(jnp.concatenate(small), ("dp", "seq"))
    small_sums = unpacked(sums, small)
    big_sums = []
    for grad in big:
        part = lax.psum_scatter(
            grad.astype(low_type), ("dp", "seq"), scatter_dimension=0, tiled=True
        )
        big_sums.append(lax.all_gather(part, ("dp", "seq"), axis=0, tiled=True).astype(f32))
    every = []
    for grad in local_grads:
        every.append(big_sums.pop(0) if grad.ndim == 2 else small_sums[0])
        small_sums = small_sums if grad.ndim == 2 else small_sums[1:]
    return (
        layer_out,
        d_x,
        every[0],
        every[1],
        every[2],
        every[3],
        every[4],
        every[5],
        every[6],
        every[7],
        every[8],
        every[9],
        every[10],
        every[11],
        every[12],
        every[13],
        every[14],
    )


def solution(mesh):
    return jax.shard_map(
        body,
        mesh=mesh,
        in_specs=(
            P(("dp", "seq"), None, None),
            P(("dp", "seq")),
            P(("dp", "seq"), None, None),
            P(),
            P(),
            P(),
            P(),
            P(),
            P(),
            P(),
            P(),
            P(),
            P(),
            P(),
            P(),
            P(),
            P(),
            P(),
        ),
        out_specs=(
            P(("dp", "seq"), None, None),
            P(("dp", "seq"), None, None),
            P(),
            P(),
            P(),
            P(),
            P(),
            P(),
            P(),
            P(),
            P(),
            P(),
            P(),
            P(),
            P(),
            P(),
            P(),
        ),
        check_vma=False,
    )
```

profile of v0, /device:TPU:0, one launch (start us, length us, event | category | flops | bytes accessed | tf_op | source)
XLA Modules:
  0.0 1139.7 jit_solution(12008616428699110538)
XLA Ops:
  55.6 23.9 %multiply_convert_fusion.1 = (bf16[640,3072]{1,0:T(8,128)(2,1)S(1)}, f32[640,3072]{1,0:T(8,128)}, f32[640,3072]{1,0:T(8,128)}) fusion(f32[3072]{0:T(1024)S(1)} %copy-done.22, bf16[768,3072]{1,0:T(8,128)(2,1)} %param.30, f32[640,768]{1,0:T(8,128)} %copy-done.8, f32[768]{0:T(1024)S(1)} %copy-done.26, f32[768]{0:T(1024)S(1)} %copy-done.19, ...), kind=kOutput, calls=%fused_computation.7 | convolution fusion | flops 3152117760 | bytes 26369024 | tf_op jit(solution)/shard_map/dot_general | solution.py:131
  79.5 7.2 fusion.47
  93.5 11.6 %convert_reduce_fusion = (f32[3072]{0:T(1024)S(1)}, bf16[640,3072]{1,0:T(8,128)(2,1)S(1)}) fusion(f32[640,3072]{1,0:T(8,128)} %get-tuple-element.64, bf16[3072,768]{1,0:T(8,128)(2,1)} %param.32, f32[640,768]{1,0:T(8,128)S(1)} %get-tuple-element.60, f32[640,3072]{1,0:T(8,128)} %get-tuple-element.80, f32[3072]{0:T(1024)S(1)} %copy-done.22), kind=kOutput, calls=%fused_computation.2 | convolution fusion | flops 3053810688 | bytes 26370048 | tf_op jit(solution)/shard_map/dot_general | solution.py:36
  117.0 4.6 copy.82
  121.6 7.5 multiply_reduce_fusion
  129.1 4.9 multiply_convert_fusion
  157.8 5.5 convert_reduce_fusion.1
  176.2 9.1 convolution_convert_fusion.1
  185.3 8.8 convolution_convert_fusion
  194.3 49.8 %reduce-scatter.19.cloned.1.call-done = bf16[24,768]{1,0:T(8,128)(2,1)} async-done(((bf16[768,768]{1,0:T(8,128)(2,1)}), bf16[24,768]{1,0:T(8,128)(2,1)}) %reduce-scatter.19.cloned.1.call-update) | async-done | bytes 36880 | tf_op jit(solution)/shard_map/reduce_scatter | solution.py:210
  244.2 100.9 %reduce-scatter.21.cloned.1.call-done = bf16[24,768]{1,0:T(8,128)(2,1)} async-done(((bf16[768,768]{1,0:T(8,128)(2,1)}), bf16[24,768]{1,0:T(8,128)(2,1)}) %reduce-scatter.21.cloned.1.call-update) | async-done | bytes 36880 | tf_op jit(solution)/shard_map/reduce_scatter | solution.py:210
  345.1 100.4 %reduce-scatter.23.cloned.1.call-done = bf16[24,768]{1,0:T(8,128)(2,1)} async-done(((bf16[768,768]{1,0:T(8,128)(2,1)}), bf16[24,768]{1,0:T(8,128)(2,1)}) %reduce-scatter.23.cloned.1.call-update) | async-done | bytes 36880 | tf_op jit(solution)/shard_map/reduce_scatter | solution.py:210
  445.6 100.8 %reduce-scatter.13.cloned.1.call-done = bf16[24,768]{1,0:T(8,128)(2,1)} async-done(((bf16[768,768]{1,0:T(8,128)(2,1)}), bf16[24,768]{1,0:T(8,128)(2,1)}) %reduce-scatter.13.cloned.1.call-update) | async-done | bytes 36880 | tf_op jit(solution)/shard_map/reduce_scatter | solution.py:210
  546.4 111.9 %reduce-scatter.15.cloned.1.call-done = bf16[24,3072]{1,0:T(8,128)(2,1)} async-done(((bf16[768,3072]{1,0:T(8,128)(2,1)}), bf16[24,3072]{1,0:T(8,128)(2,1)}) %reduce-scatter.15.cloned.1.call-update) | async-done | bytes 147472 | tf_op jit(solution)/shard_map/reduce_scatter | solution.py:210
  658.4 112.9 %reduce-scatter.17.cloned.1.call-done = bf16[96,768]{1,0:T(8,128)(2,1)} async-done(((bf16[3072,768]{1,0:T(8,128)(2,1)}), bf16[96,768]{1,0:T(8,128)(2,1)}) %reduce-scatter.17.cloned.1.call-update) | async-done | bytes 147472 | tf_op jit(solution)/shard_map/reduce_scatter | solution.py:210
  771.5 40.6 %psum.7 = f32[9216]{0:T(1024)S(1)} all-reduce(f32[9216]{0:T(1024)S(1)} %constant_dynamic-update-slice_fusion), channel_id=1, replica_groups=mesh['dp'=16,'seq'=2] {'dp','seq'}, use_global_device_ids=true, to_apply=%region_21.22 | all-reduce | flops 9216 | bytes 73728 | tf_op jit(solution)/shard_map/psum | solution.py:206
  820.0 7.2 all-gather.7.cloned.1.call-done
  830.1 53.1 %all-gather.9.cloned.1.call-done = bf16[768,768]{1,0:T(8,128)(2,1)} async-done(((bf16[24,768]{1,0:T(8,128)(2,1)}), bf16[768,768]{1,0:T(8,128)(2,1)}) %all-gather.9.cloned.1.call-update) | async-done | bytes 1179664 | tf_op jit(solution)/shard_map/all_gather | solution.py:213
  886.0 53.1 %all-gather.11.cloned.1.call-done = bf16[768,768]{1,0:T(8,128)(2,1)} async-done(((bf16[24,768]{1,0:T(8,128)(2,1)}), bf16[768,768]{1,0:T(8,128)(2,1)}) %all-gather.11.cloned.1.call-update) | async-done | bytes 1179664 | tf_op jit(solution)/shard_map/all_gather | solution.py:213
  941.9 52.9 %all-gather.13.cloned.1.call-done = bf16[768,768]{1,0:T(8,128)(2,1)} async-done(((bf16[24,768]{1,0:T(8,128)(2,1)}), bf16[768,768]{1,0:T(8,128)(2,1)}) %all-gather.13.cloned.1.call-update) | async-done | bytes 1179664 | tf_op jit(solution)/shard_map/all_gather | solution.py:213
  997.7 62.7 %all-gather.15.cloned.1.call-done = bf16[768,3072]{1,0:T(8,128)(2,1)} async-done(((bf16[24,3072]{1,0:T(8,128)(2,1)}), bf16[768,3072]{1,0:T(8,128)(2,1)}) %all-gather.15.cloned.1.call-update) | async-done | bytes 4718608 | tf_op jit(solution)/shard_map/all_gather | solution.py:213
  1060.4 7.4 convert_element_type.217
  1067.7 57.9 %all-gather.17.cloned.1.call-done = bf16[3072,768]{1,0:T(8,128)(2,1)} async-done(((bf16[96,768]{1,0:T(8,128)(2,1)}), bf16[3072,768]{1,0:T(8,128)(2,1)}) %all-gather.17.cloned.1.call-update) | async-done | bytes 4718608 | tf_op jit(solution)/shard_map/all_gather | solution.py:213
  1125.6 6.8 convert_element_type.219
  (158 shorter events, 123.0 us)
Async XLA Ops:
  7.2 43.9 %copy-start = (bf16[768,768]{1,0:T(8,128)(2,1)S(1)}, bf16[768,768]{1,0:T(8,128)(2,1)}, u32[]{:S(2)}) copy-start(bf16[768,768]{1,0:T(8,128)(2,1)} %param.26) | copy-start | bytes 3538948
  7.2 236.9 %reduce-scatter.19.cloned.1.call-start = ((), (), s32[]{:S(2)}) async-start(), calls=%async_computation.15 | async-start | bytes 1216512 | tf_op jit(solution)/shard_map/reduce_scatter | solution.py:210
  12.5 4.6 copy-start.20
  12.5 4.6 copy-start.23
  44.6 6.5 copy-start.24
  55.5 24.0 %copy-start.9 = (f32[640,768]{1,0:T(8,128)S(1)}, f32[640,768]{1,0:T(8,128)}, u32[]{:S(2)}) copy-start(f32[640,768]{1,0:T(8,128)} %copy-done.8) | copy-start | bytes 5898244
  55.5 24.0 %copy-start.25 = (f32[768]{0:T(1024)S(1)}, f32[768]{0:T(1024)}, u32[]{:S(2)}) copy-start(f32[768]{0:T(1024)} %param.33) | copy-start | bytes 9220
  79.5 7.2 copy-start.27
  79.5 7.6 copy-start.17
  90.2 15.0 %slice-start = ((s8[4718592]{0:T(1024)(128)(4,1)}), s8[4194304]{0:T(1024)(128)(4,1)S(1)}, s32[]{:S(2)}) async-start(s8[4718592]{0:T(1024)(128)(4,1)} %bitcast.81), calls=%async_computation.18 | async-start | bytes 8388608
  93.5 11.7 %copy-start.14 = (f32[640,768]{1,0:T(8,128)}, f32[640,768]{1,0:T(8,128)S(1)}, u32[]{:S(2)}) copy-start(f32[640,768]{1,0:T(8,128)S(1)} %get-tuple-element.60) | copy-start | bytes 5898244
  93.5 11.7 %copy-start.10 = (f32[640,768]{1,0:T(8,128)S(1)}, f32[640,768]{1,0:T(8,128)}, u32[]{:S(2)}) copy-start(f32[640,768]{1,0:T(8,128)} %copy-done.8) | copy-start | bytes 5898244
  93.5 11.7 %slice-start.1 = ((s8[4718592]{0:T(1024)(128)(4,1)}), s8[524288]{0:T(1024)(128)(4,1)S(1)}, s32[]{:S(2)}) async-start(s8[4718592]{0:T(1024)(128)(4,1)} %bitcast.81), calls=%async_computation.19 | async-start | bytes 1048576
  145.0 200.0 %reduce-scatter.21.cloned.1.call-start = ((), (), s32[]{:S(2)}) async-start(), calls=%async_computation.16 | async-start | bytes 1216512 | tf_op jit(solution)/shard_map/reduce_scatter | solution.py:210
  157.7 287.8 %reduce-scatter.23.cloned.1.call-start = ((), (), s32[]{:S(2)}) async-start(), calls=%async_computation.17 | async-start | bytes 1216512 | tf_op jit(solution)/shard_map/reduce_scatter | solution.py:210
  172.7 373.6 %reduce-scatter.13.cloned.1.call-start = ((), (), s32[]{:S(2)}) async-start(), calls=%async_computation.9 | async-start | bytes 1216512 | tf_op jit(solution)/shard_map/reduce_scatter | solution.py:210
  176.1 482.2 %reduce-scatter.15.cloned.1.call-start = ((), (), s32[]{:S(2)}) async-start(), calls=%async_computation.11 | async-start | bytes 4866048 | tf_op jit(solution)/shard_map/reduce_scatter | solution.py:210
  185.3 585.9 %reduce-scatter.17.cloned.1.call-start = ((), (), s32[]{:S(2)}) async-start(), calls=%async_computation.13 | async-start | bytes 4866048 | tf_op jit(solution)/shard_map/reduce_scatter | solution.py:210
  194.2 633.1 %all-gather.7.cloned.1.call-start = ((), (), s32[]{:S(2)}) async-start(), calls=%async_computation.6 | async-start | bytes 1216512 | tf_op jit(solution)/shard_map/all_gather | solution.py:213
  244.1 639.1 %all-gather.9.cloned.1.call-start = ((), (), s32[]{:S(2)}) async-start(), calls=%async_computation.7 | async-start | bytes 1216512 | tf_op jit(solution)/shard_map/all_gather | solution.py:213
  345.0 594.0 %all-gather.11.cloned.1.call-start = ((), (), s32[]{:S(2)}) async-start(), calls=%async_computation.8 | async-start | bytes 1216512 | tf_op jit(solution)/shard_map/all_gather | solution.py:213
  445.5 549.3 %all-gather.13.cloned.1.call-start = ((), (), s32[]{:S(2)}) async-start(), calls=%async_computation.10 | async-start | bytes 1216512 | tf_op jit(solution)/shard_map/all_gather | solution.py:213
  546.3 514.0 %all-gather.15.cloned.1.call-start = ((), (), s32[]{:S(2)}) async-start(), calls=%async_computation.12 | async-start | bytes 4866048 | tf_op jit(solution)/shard_map/all_gather | solution.py:213
  658.3 467.3 %all-gather.17.cloned.1.call-start = ((), (), s32[]{:S(2)}) async-start(), calls=%async_computation.14 | async-start | bytes 4866048 | tf_op jit(solution)/shard_map/all_gather | solution.py:213
  (19 other events, 53.4 us)
Sparse Core Ops, SparseCore 0:
  145.2 98.8 reduce-scatter.18
  249.7 95.2 reduce-scatter.20
  350.1 95.3 reduce-scatter.22
  451.0 95.2 reduce-scatter.12
  552.2 106.0 reduce-scatter.14
  665.1 106.0 reduce-scatter.16
  774.1 53.1 all-gather.6
  830.2 52.9 all-gather.8
  886.1 52.9 all-gather.10
  941.8 52.9 all-gather.12
  997.7 62.5 all-gather.14
  1063.1 62.4 all-gather.16
where the time goes:
time: 1150 us; the launch traced here: 1140 us
  waiting for transfers between devices  864 us (75%)
  matrix products  120 us (10%)
  local copies, waits for them, and re-layouts  60.8 us (5%)
  blocking collectives  40.6 us (4%)
  other arithmetic  38.7 us (3%)
  between operations  15.3 us (1%)
    reduce_scatter x6, waiting for transfers between devices, body(): lax.psum_scatter(grad.astype(low_type), ('dp', 'seq'), scatter_dimension=...  577 us
    all_gather x6, waiting for transfers between devices, body(): lax.all_gather(part, ('dp', 'seq'), axis=0, tiled=True).astype(f32)  287 us
    psum x1, blocking collectives, body(): sums = lax.psum(jnp.concatenate(small), ('dp', 'seq'))  40.6 us
    dot_general x6, matrix products, over_rows(): lax.dot_general(left, right, (((0,), (0,)), ((), ())), preferred_element_...  32.1 us
    convert_element_type x6, other arithmetic, body(): lax.all_gather(part, ('dp', 'seq'), axis=0, tiled=True).astype(f32)  25.6 us
    dot_general x1, matrix products, body(): pre = jnp.dot(fin, w_inner, preferred_element_type=f32) + b_inner  23.9 us
    dot_general x6, matrix products, times_trans(): lax.dot_general(left, weight, (((1,), (1,)), ((), ())), preferred_element...  23.5 us
  transfers between devices with their start and end apart: 12, of which 12 were waited for; matrix products, arithmetic and copies ran while one was open for 7% of the time, Pallas kernels for 0%

commit v1 on v0

--- a/solution.py
+++ b/solution.py
@@ -2,9 +2,36 @@
 import jax.numpy as jnp
 from jax import lax
 from jax.sharding import PartitionSpec as P
+from jax.lax import axis_index, axis_size, ppermute
 
 H = 12
 EPS = 1e-12
+
+
+def resolve_column(t0, dim_at):
+    spare = list(t0.shape[1:])
+    spare[dim_at] *= t0.shape[0]
+    return jnp.moveaxis(t0, 0, dim_at).reshape(spare)
+
+
+def _remake_trails(panel, comm_axis):
+    z_new = axis_size(comm_axis)
+    current_block = axis_index(comm_axis)
+    y1, view_out = (z_new, current_block)
+    current_value, local_part = (panel[None], 1)
+    while local_part < y1:
+        tile_out = ppermute(current_value, comm_axis, [(k0, k0 ^ local_part) for k0 in range(y1)])
+        before = view_out & local_part == 0
+        near = jnp.where(before, current_value, tile_out)
+        t1 = jnp.where(before, tile_out, current_value)
+        current_value = jnp.concatenate([near, t1])
+        local_part *= 2
+    return current_value
+
+
+def arrange_ends(work_x, row_data, axis_k):
+    front = _remake_trails(work_x, row_data)
+    return resolve_column(front, axis_k)
 
 
 def norm_forward(h, gain, shift):
@@ -210,7 +237,7 @@
         part = lax.psum_scatter(
             grad.astype(low_type), ("dp", "seq"), scatter_dimension=0, tiled=True
         )
-        big_sums.append(lax.all_gather(part, ("dp", "seq"), axis=0, tiled=True).astype(f32))
+        big_sums.append(arrange_ends(part, ("dp", "seq"), 0).astype(f32))
     every = []
     for grad in local_grads:
         every.append(big_sums.pop(0) if grad.ndim == 2 else small_sums[0])

time: 1150 us -> 1040 us (0.904)
  waiting for transfers between devices: 864 us -> 708 us
  starting transfers between devices: 0.48 us -> 33.9 us
    reduce_scatter x6 -> x2, waiting for transfers between devices: 577 us -> 147 us  [body(): lax.psum_scatter(grad.astype(low_type), ('dp', 'seq'), scatter_dimension=...]
    unnamed x12 -> x10, waiting for transfers between devices: 0.2 us -> 296 us
    all_gather x6 -> x0, waiting for transfers between devices: 287 us -> none  [body(): lax.all_gather(part, ('dp', 'seq'), axis=0, tiled=True).astype(f32)]
    ppermute x0 -> x30, waiting for transfers between devices: none -> 264 us  [_remake_trails(): ppermute(current_value, comm_axis, [(k0, k0 ^ local_part) for k0 in range...]
    ppermute x0 -> x30, starting transfers between devices: none -> 33.3 us  [_remake_trails(): ppermute(current_value, comm_axis, [(k0, k0 ^ local_part) for k0 in range...]
  transfers between devices with their start and end apart: 12 -> 36, of which waited for: 12 -> 18; matrix products, arithmetic and copies ran while one was open for 7% -> 9% of each run, Pallas kernels for 0% -> 0%
where the time goes in v1:
time: 1040 us; the launch traced here: 1030 us
  waiting for transfers between devices  708 us (68%)
  matrix products  123 us (12%)
  local copies, waits for them, and re-layouts  61.7 us (6%)
  other arithmetic  44 us (4%)
  blocking collectives  42.7 us (4%)
  starting transfers between devices  33.9 us (3%)
  between operations  15.6 us (2%)
    unnamed x10, waiting for transfers between devices  296 us
    ppermute x30, waiting for transfers between devices, _remake_trails(): ppermute(current_value, comm_axis, [(k0, k0 ^ local_part) for k0 in range...  264 us
    reduce_scatter x2, waiting for transfers between devices, body(): lax.psum_scatter(grad.astype(low_type), ('dp', 'seq'), scatter_dimension=...  147 us
    psum x1, blocking collectives, body(): sums = lax.psum(jnp.concatenate(small), ('dp', 'seq'))  42.7 us
    ppermute x30, starting transfers between devices, _remake_trails(): ppermute(current_value, comm_axis, [(k0, k0 ^ local_part) for k0 in range...  33.3 us
    dot_general x6, matrix products, over_rows(): lax.dot_general(left, right, (((0,), (0,)), ((), ())), preferred_element_...  29.8 us
    dot_general x6, matrix products, times_trans(): lax.dot_general(left, weight, (((1,), (1,)), ((), ())), preferred_element...  28.1 us
    dot_general x1, matrix products, body(): pre = jnp.dot(fin, w_inner, preferred_element_type=f32) + b_inner  23.9 us
  transfers between devices with their start and end apart: 36, of which 18 were waited for; matrix products, arithmetic and copies ran while one was open for 9% of the time, Pallas kernels for 0%

profile of v1, /device:TPU:0, one launch (start us, length us, event | category | flops | bytes accessed | tf_op | source)
XLA Modules:
  0.0 1028.4 jit_solution(13648942431396842699)
XLA Ops:
  55.5 23.9 %multiply_convert_fusion.1 = (bf16[640,3072]{1,0:T(8,128)(2,1)S(1)}, f32[640,3072]{1,0:T(8,128)}, f32[640,3072]{1,0:T(8,128)}) fusion(f32[3072]{0:T(1024)S(1)} %copy-done.25, bf16[768,3072]{1,0:T(8,128)(2,1)} %param.30, f32[640,768]{1,0:T(8,128)} %copy-done.9, f32[768]{0:T(1024)S(1)} %copy-done.29, f32[768]{0:T(1024)S(1)} %copy-done.22, ...), kind=kOutput, calls=%fused_computation.7 | convolution fusion | flops 3152117760 | bytes 26369024 | tf_op jit(solution)/shard_map/dot_general | solution.py:158
  79.5 7.2 fusion.47
  93.4 11.3 %convert_reduce_fusion = (f32[3072]{0:T(1024)S(1)}, bf16[640,3072]{1,0:T(8,128)(2,1)S(1)}) fusion(f32[640,3072]{1,0:T(8,128)} %get-tuple-element.30, bf16[3072,768]{1,0:T(8,128)(2,1)} %param.32, f32[640,768]{1,0:T(8,128)S(1)} %get-tuple-element.26, f32[640,3072]{1,0:T(8,128)} %get-tuple-element.106, f32[3072]{0:T(1024)S(1)} %copy-done.25), kind=kOutput, calls=%fused_computation.2 | convolution fusion | flops 3053810688 | bytes 26370048 | tf_op jit(solution)/shard_map/dot_general | solution.py:63
  121.2 7.5 multiply_reduce_fusion
  128.7 5.1 multiply_convert_fusion
  153.7 5.5 convert_reduce_fusion.1
  170.8 9.1 convolution_convert_fusion.1
  180.2 8.9 convolution_convert_fusion
  195.6 42.7 %psum.7 = f32[9216]{0:T(1024)S(1)} all-reduce(f32[9216]{0:T(1024)S(1)} %constant_dynamic-update-slice_fusion), channel_id=1, replica_groups=mesh['dp'=16,'seq'=2] {'dp','seq'}, use_global_device_ids=true, to_apply=%region_21.22 | all-reduce | flops 9216 | bytes 73728 | tf_op jit(solution)/shard_map/psum | solution.py:233
  238.3 4.8 add_add_fusion
  245.3 97.6 %reduce-scatter.21.cloned.1.call-done = bf16[24,768]{1,0:T(8,128)(2,1)} async-done(((bf16[768,768]{1,0:T(8,128)(2,1)}), bf16[24,768]{1,0:T(8,128)(2,1)}) %reduce-scatter.21.cloned.1.call-update) | async-done | bytes 36880
  343.9 99.4 %reduce-scatter.23.cloned.1.call-done = bf16[24,768]{1,0:T(8,128)(2,1)} async-done(((bf16[768,768]{1,0:T(8,128)(2,1)}), bf16[24,768]{1,0:T(8,128)(2,1)}) %reduce-scatter.23.cloned.1.call-update) | async-done | bytes 36880
  444.4 99.3 %reduce-scatter.25.cloned.1.call-done = bf16[24,768]{1,0:T(8,128)(2,1)} async-done(((bf16[768,768]{1,0:T(8,128)(2,1)}), bf16[24,768]{1,0:T(8,128)(2,1)}) %reduce-scatter.25.cloned.1.call-update) | async-done | bytes 36880
  568.8 19.4 %collective-permute-done.8 = bf16[8,24,768]{2,1,0:T(8,128)(2,1)S(1)} collective-permute-done((bf16[8,24,768]{2,1,0:T(8,128)(2,1)S(1)}, bf16[8,24,768]{2,1,0:T(8,128)(2,1)S(1)}, u32[]{:S(2)}, u32[]{:S(2)}) %collective-permute-start.8) | collective-permute-done | bytes 294944 | tf_op jit(solution)/shard_map/ppermute | solution.py:23
  589.1 78.0 %reduce-scatter.15.cloned.1.call-done = bf16[24,3072]{1,0:T(8,128)(2,1)} async-done(((bf16[768,3072]{1,0:T(8,128)(2,1)}), bf16[24,3072]{1,0:T(8,128)(2,1)}) %reduce-scatter.15.cloned.1.call-update) | async-done | bytes 147472 | tf_op jit(solution)/shard_map/reduce_scatter | solution.py:237
  683.7 26.9 %collective-permute-done.14 = bf16[16,24,768]{2,1,0:T(8,128)(2,1)S(1)} collective-permute-done((bf16[16,24,768]{2,1,0:T(8,128)(2,1)S(1)}, bf16[16,24,768]{2,1,0:T(8,128)(2,1)S(1)}, u32[]{:S(2)}, u32[]{:S(2)}) %collective-permute-start.14) | collective-permute-done | bytes 589856 | tf_op jit(solution)/shard_map/ppermute | solution.py:23
  710.7 69.3 %reduce-scatter.17.cloned.1.call-done = bf16[96,768]{1,0:T(8,128)(2,1)} async-done(((bf16[3072,768]{1,0:T(8,128)(2,1)}), bf16[96,768]{1,0:T(8,128)(2,1)}) %reduce-scatter.17.cloned.1.call-update) | async-done | bytes 147472 | tf_op jit(solution)/shard_map/reduce_scatter | solution.py:237
  785.8 6.3 collective-permute-done.26
  793.8 16.0 %collective-permute-done.23 = bf16[8,24,3072]{2,1,0:T(8,128)(2,1)S(1)} collective-permute-done((bf16[8,24,3072]{2,1,0:T(8,128)(2,1)S(1)}, bf16[8,24,3072]{2,1,0:T(8,128)(2,1)S(1)}, u32[]{:S(2)}, u32[]{:S(2)}) %collective-permute-start.23) | collective-permute-done | bytes 1179680 | tf_op jit(solution)/shard_map/ppermute | solution.py:23
  818.6 68.9 %collective-permute-done.28 = bf16[8,96,768]{2,1,0:T(8,128)(2,1)S(1)} collective-permute-done((bf16[8,96,768]{2,1,0:T(8,128)(2,1)S(1)}, bf16[8,96,768]{2,1,0:T(8,128)(2,1)S(1)}, u32[]{:S(2)}, u32[]{:S(2)}) %collective-permute-start.28) | collective-permute-done | bytes 1179680 | tf_op jit(solution)/shard_map/ppermute | solution.py:23
  892.7 73.3 %collective-permute-done.24 = bf16[16,24,3072]{2,1,0:T(8,128)(2,1)S(1)} collective-permute-done((bf16[16,24,3072]{2,1,0:T(8,128)(2,1)S(1)}, bf16[16,24,3072]{2,1,0:T(8,128)(2,1)S(1)}, u32[]{:S(2)}, u32[]{:S(2)}) %collective-permute-start.24) | collective-permute-done | bytes 2359328 | tf_op jit(solution)/shard_map/ppermute | solution.py:23
  966.7 5.3 bitcast_convert_fusion.1
  972.0 43.6 %collective-permute-done.29 = bf16[16,96,768]{2,1,0:T(8,128)(2,1)S(1)} collective-permute-done((bf16[16,96,768]{2,1,0:T(8,128)(2,1)S(1)}, bf16[16,96,768]{2,1,0:T(8,128)(2,1)S(1)}, u32[]{:S(2)}, u32[]{:S(2)}) %collective-permute-start.29) | collective-permute-done | bytes 2359328 | tf_op jit(solution)/shard_map/ppermute | solution.py:23
  1016.3 4.8 bitcast_convert_fusion
  (278 shorter events, 178.6 us)
Async XLA Ops:
  7.2 235.8 %reduce-scatter.19.cloned.1.call-start = ((), (), s32[]{:S(2)}) async-start(), calls=%async_computation.8 | async-start | bytes 1216512
  142.9 200.1 %reduce-scatter.21.cloned.1.call-start = ((), (), s32[]{:S(2)}) async-start(), calls=%async_computation.9 | async-start | bytes 1216512
  153.5 289.9 %reduce-scatter.23.cloned.1.call-start = ((), (), s32[]{:S(2)}) async-start(), calls=%async_computation.10 | async-start | bytes 1216512
  167.4 376.3 %reduce-scatter.25.cloned.1.call-start = ((), (), s32[]{:S(2)}) async-start(), calls=%async_computation.11 | async-start | bytes 1216512
  170.8 496.4 %reduce-scatter.15.cloned.1.call-start = ((), (), s32[]{:S(2)}) async-start(), calls=%async_computation.6 | async-start | bytes 4866048 | tf_op jit(solution)/shard_map/reduce_scatter | solution.py:237
  179.9 600.1 %reduce-scatter.17.cloned.1.call-start = ((), (), s32[]{:S(2)}) async-start(), calls=%async_computation.7 | async-start | bytes 4866048 | tf_op jit(solution)/shard_map/reduce_scatter | solution.py:237
  244.0 300.7 %collective-permute-start = (bf16[1,24,768]{1,2,0:T(8,128)(2,1)S(1)}, bf16[1,24,768]{1,2,0:T(8,128)(2,1)S(1)}, u32[]{:S(2)}, u32[]{:S(2)}) collective-permute-start(bf16[1,24,768]{1,2,0:T(8,128)(2,1)S(1)} %bitcast.118), channel_id=1, source_target_pairs={{0,1},{1,0},{2,3},{3,2},{4,5},{5,4},{6,7},{7,6},{8,9},{9,8},{10,11... | collective-permute-start | bytes 110600 | tf_op jit(solution)/shard_map/ppermute | solution.py:23
  343.9 202.6 %collective-permute-start.5 = (bf16[1,24,768]{1,2,0:T(8,128)(2,1)S(1)}, bf16[1,24,768]{1,2,0:T(8,128)(2,1)S(1)}, u32[]{:S(2)}, u32[]{:S(2)}) collective-permute-start(bf16[1,24,768]{1,2,0:T(8,128)(2,1)S(1)} %bitcast.121), channel_id=1, source_target_pairs={{0,1},{1,0},{2,3},{3,2},{4,5},{5,4},{6,7},{7,6},{8,9},{9,8},{10,11... | collective-permute-start | bytes 110600 | tf_op jit(solution)/shard_map/ppermute | solution.py:23
  444.3 103.1 %collective-permute-start.10 = (bf16[1,24,768]{1,2,0:T(8,128)(2,1)S(1)}, bf16[1,24,768]{1,2,0:T(8,128)(2,1)S(1)}, u32[]{:S(2)}, u32[]{:S(2)}) collective-permute-start(bf16[1,24,768]{1,2,0:T(8,128)(2,1)S(1)} %bitcast.120), channel_id=1, source_target_pairs={{0,1},{1,0},{2,3},{3,2},{4,5},{5,4},{6,7},{7,6},{8,9},{9,8},{10,11... | collective-permute-start | bytes 110600 | tf_op jit(solution)/shard_map/ppermute | solution.py:23
  555.1 10.3 %collective-permute-start.17 = (bf16[4,24,768]{2,1,0:T(8,128)(2,1)S(1)}, bf16[4,24,768]{2,1,0:T(8,128)(2,1)S(1)}, u32[]{:S(2)}, u32[]{:S(2)}) collective-permute-start(bf16[4,24,768]{2,1,0:T(8,128)(2,1)S(1)} %pad_maximum_fusion.25), channel_id=1, source_target_pairs={{0,4},{1,5},{2,6},{3,7},{4,0},{5,1},{6,2},{7,3},{8,12},{9,13},{10,... | collective-permute-start | bytes 442376 | tf_op jit(solution)/shard_map/ppermute | solution.py:23
  557.1 10.0 collective-permute-start.3
  560.3 27.9 %collective-permute-start.8 = (bf16[8,24,768]{2,1,0:T(8,128)(2,1)S(1)}, bf16[8,24,768]{2,1,0:T(8,128)(2,1)S(1)}, u32[]{:S(2)}, u32[]{:S(2)}) collective-permute-start(bf16[8,24,768]{2,1,0:T(8,128)(2,1)S(1)} %pad_maximum_fusion.17), channel_id=1, source_target_pairs={{0,8},{1,9},{2,10},{3,11},{4,12},{5,13},{6,14},{7,15},{8,0},{9,1},... | collective-permute-start | bytes 884744 | tf_op jit(solution)/shard_map/ppermute | solution.py:23
  564.1 103.1 %collective-permute-start.13 = (bf16[8,24,768]{2,1,0:T(8,128)(2,1)}, bf16[8,24,768]{2,1,0:T(8,128)(2,1)}, u32[]{:S(2)}, u32[]{:S(2)}) collective-permute-start(bf16[8,24,768]{2,1,0:T(8,128)(2,1)} %pad_maximum_fusion.18), channel_id=1, source_target_pairs={{0,8},{1,9},{2,10},{3,11},{4,12},{5,13},{6,14},{7,15},{8,0},{9,1},... | collective-permute-start | bytes 884744 | tf_op jit(solution)/shard_map/ppermute | solution.py:23
  565.5 105.9 %collective-permute-start.18 = (bf16[8,24,768]{2,1,0:T(8,128)(2,1)S(1)}, bf16[8,24,768]{2,1,0:T(8,128)(2,1)}, u32[]{:S(2)}, u32[]{:S(2)}) collective-permute-start(bf16[8,24,768]{2,1,0:T(8,128)(2,1)S(1)} %pad_maximum_fusion.19), channel_id=1, source_target_pairs={{0,8},{1,9},{2,10},{3,11},{4,12},{5,13},{6,14},{7,15},{8,0},{9,1},... | collective-permute-start | bytes 884744 | tf_op jit(solution)/shard_map/ppermute | solution.py:23
  567.3 114.2 %collective-permute-start.4 = (bf16[16,24,768]{2,1,0:T(8,128)(2,1)S(1)}, bf16[16,24,768]{2,1,0:T(8,128)(2,1)S(1)}, u32[]{:S(2)}, u32[]{:S(2)}) collective-permute-start(bf16[16,24,768]{2,1,0:T(8,128)(2,1)S(1)} %pad_maximum_fusion.10), channel_id=1, source_target_pairs={{0,16},{1,17},{2,18},{3,19},{4,20},{5,21},{6,22},{7,23},{8,24},{9,... | collective-permute-start | bytes 1769480 | tf_op jit(solution)/shard_map/ppermute | solution.py:23
  589.1 93.4 %collective-permute-start.9 = (bf16[16,24,768]{2,1,0:T(8,128)(2,1)}, bf16[16,24,768]{2,1,0:T(8,128)(2,1)}, u32[]{:S(2)}, u32[]{:S(2)}) collective-permute-start(bf16[16,24,768]{2,1,0:T(8,128)(2,1)} %pad_maximum_fusion.11), channel_id=1, source_target_pairs={{0,16},{1,17},{2,18},{3,19},{4,20},{5,21},{6,22},{7,23},{8,24},{9,... | collective-permute-start | bytes 1769480 | tf_op jit(solution)/shard_map/ppermute | solution.py:23
  668.3 42.4 %collective-permute-start.14 = (bf16[16,24,768]{2,1,0:T(8,128)(2,1)S(1)}, bf16[16,24,768]{2,1,0:T(8,128)(2,1)S(1)}, u32[]{:S(2)}, u32[]{:S(2)}) collective-permute-start(bf16[16,24,768]{2,1,0:T(8,128)(2,1)S(1)} %pad_maximum_fusion.12), channel_id=1, source_target_pairs={{0,16},{1,17},{2,18},{3,19},{4,20},{5,21},{6,22},{7,23},{8,24},{9,... | collective-permute-start | bytes 1769480 | tf_op jit(solution)/shard_map/ppermute | solution.py:23
  673.3 111.4 %collective-permute-start.19 = (bf16[16,24,768]{2,1,0:T(8,128)(2,1)}, bf16[16,24,768]{2,1,0:T(8,128)(2,1)}, u32[]{:S(2)}, u32[]{:S(2)}) collective-permute-start(bf16[16,24,768]{2,1,0:T(8,128)(2,1)} %pad_maximum_fusion.13), channel_id=1, source_target_pairs={{0,16},{1,17},{2,18},{3,19},{4,20},{5,21},{6,22},{7,23},{8,24},{9,... | collective-permute-start | bytes 1769480 | tf_op jit(solution)/shard_map/ppermute | solution.py:23
  680.0 100.0 %collective-permute-start.22 = (bf16[4,24,3072]{2,1,0:T(8,128)(2,1)}, bf16[4,24,3072]{2,1,0:T(8,128)(2,1)}, u32[]{:S(2)}, u32[]{:S(2)}) collective-permute-start(bf16[4,24,3072]{2,1,0:T(8,128)(2,1)} %pad_maximum_fusion.14), channel_id=1, source_target_pairs={{0,4},{1,5},{2,6},{3,7},{4,0},{5,1},{6,2},{7,3},{8,12},{9,13},{10,... | collective-permute-start | bytes 1769480 | tf_op jit(solution)/shard_map/ppermute | solution.py:23
  781.4 28.4 %collective-permute-start.23 = (bf16[8,24,3072]{2,1,0:T(8,128)(2,1)S(1)}, bf16[8,24,3072]{2,1,0:T(8,128)(2,1)S(1)}, u32[]{:S(2)}, u32[]{:S(2)}) collective-permute-start(bf16[8,24,3072]{2,1,0:T(8,128)(2,1)S(1)} %pad_maximum_fusion.8), channel_id=1, source_target_pairs={{0,8},{1,9},{2,10},{3,11},{4,12},{5,13},{6,14},{7,15},{8,0},{9,1},... | collective-permute-start | bytes 3538952 | tf_op jit(solution)/shard_map/ppermute | solution.py:23
  792.3 19.5 %collective-permute-start.27 = (bf16[4,96,768]{2,1,0:T(8,128)(2,1)S(1)}, bf16[4,96,768]{2,1,0:T(8,128)(2,1)S(1)}, u32[]{:S(2)}, u32[]{:S(2)}) collective-permute-start(bf16[4,96,768]{2,1,0:T(8,128)(2,1)S(1)} %pad_maximum_fusion.15), channel_id=1, source_target_pairs={{0,4},{1,5},{2,6},{3,7},{4,0},{5,1},{6,2},{7,3},{8,12},{9,13},{10,... | collective-permute-start | bytes 1769480 | tf_op jit(solution)/shard_map/ppermute | solution.py:23
  810.2 155.8 %collective-permute-start.24 = (bf16[16,24,3072]{2,1,0:T(8,128)(2,1)S(1)}, bf16[16,24,3072]{2,1,0:T(8,128)(2,1)S(1)}, u32[]{:S(2)}, u32[]{:S(2)}) collective-permute-start(bf16[16,24,3072]{2,1,0:T(8,128)(2,1)S(1)} %pad_maximum_fusion.2), channel_id=1, source_target_pairs={{0,16},{1,17},{2,18},{3,19},{4,20},{5,21},{6,22},{7,23},{8,24},{9,... | collective-permute-start | bytes 7077896 | tf_op jit(solution)/shard_map/ppermute | solution.py:23
  812.0 75.4 %collective-permute-start.28 = (bf16[8,96,768]{2,1,0:T(8,128)(2,1)S(1)}, bf16[8,96,768]{2,1,0:T(8,128)(2,1)S(1)}, u32[]{:S(2)}, u32[]{:S(2)}) collective-permute-start(bf16[8,96,768]{2,1,0:T(8,128)(2,1)S(1)} %pad_maximum_fusion.9), channel_id=1, source_target_pairs={{0,8},{1,9},{2,10},{3,11},{4,12},{5,13},{6,14},{7,15},{8,0},{9,1},... | collective-permute-start | bytes 3538952 | tf_op jit(solution)/shard_map/ppermute | solution.py:23
  887.8 127.8 %collective-permute-start.29 = (bf16[16,96,768]{2,1,0:T(8,128)(2,1)S(1)}, bf16[16,96,768]{2,1,0:T(8,128)(2,1)S(1)}, u32[]{:S(2)}, u32[]{:S(2)}) collective-permute-start(bf16[16,96,768]{2,1,0:T(8,128)(2,1)S(1)} %pad_maximum_fusion.3), channel_id=1, source_target_pairs={{0,16},{1,17},{2,18},{3,19},{4,20},{5,21},{6,22},{7,23},{8,24},{9,... | collective-permute-start | bytes 7077896 | tf_op jit(solution)/shard_map/ppermute | solution.py:23
  (46 other events, 310.9 us)
Sparse Core Ops, SparseCore 0:
  143.0 98.9 reduce-scatter.18
  247.7 95.2 reduce-scatter.20
  348.0 95.2 reduce-scatter.22
  448.3 95.2 reduce-scatter.24
  549.5 117.5 reduce-scatter.14
  673.9 106.0 reduce-scatter.16
